TPU v7x, 32 devices: a whole 2x2x4 slice. The times are simulated.
32 devices in a mesh: ka: 2 (over x), band: 16 (over z, y, core).
Axes of the slice: x: 2, y: 2, z: 4, core: 2. Of those that a mesh axis runs over, the one named last changes fastest.
Arguments:
- psi_hat: float32 [2, 12, 2, 128, 128, 128], P('ka', None, None, 'band'), may hold values from -1.5 to 1.5
- occupations: int32 [2, 12], P('ka'), may hold values from 0 to 2
- weights: int32 [2], P('ka'), may hold values from 1 to 6
- density_in: float32 [128, 128, 128], P('band'), may hold values from -12 to 12
- dens_hist: float32 [8, 128, 128, 128], P(None, 'band'), may hold values from -3 to 3
- resid_hist: float32 [8, 128, 128, 128], P(None, 'band'), may hold values from -12 to 12
Outputs:
- out_density: float32 [128, 128, 128], P('band')
- mixed_density: float32 [128, 128, 128], P('band')
All inputs are finite; a program needn't handle non-finite values.
Results may differ from a plain program's by a relative error of at most 0.0003.
Values sent between devices are 32-bit elements; how exact they have to be, the bound alone decides.
A program may use at most 128 MiB of HBM per device.

v0:
```python
from functools import partial
import jax
import jax.numpy as jnp
from jax import lax
from jax.sharding import PartitionSpec as P

NG = 128
highest = lax.Precision.HIGHEST
beta_mix = 0.3
regular = 0.01


def dft_tables():
    indices = jnp.arange(NG, dtype=jnp.int32)
    product = indices[:, None] * indices[None, :] % NG
    angles = product.astype(jnp.float32) * jnp.float32(2.0 * 3.141592653589793 / NG)
    return (jnp.cos(angles), jnp.sin(angles))


def rotate(pattern, real_part, imag_part, cosine_table, sine_table):
    einsum = partial(jnp.einsum, precision=highest)
    out_real = einsum(pattern, real_part, cosine_table) - einsum(pattern, imag_part, sine_table)
    out_imag = einsum(pattern, real_part, sine_table) + einsum(pattern, imag_part, cosine_table)
    return (out_real, out_imag)


def history_gram(resid_hist):
    return jnp.einsum("hzxy,gzxy->hg", resid_hist, resid_hist, precision=highest)


def local_sums(residual_now, resid_hist):
    projections = jnp.einsum("hzxy,zxy->h", resid_hist, residual_now, precision=highest)[:, None]
    return jnp.concatenate([history_gram(resid_hist), projections], axis=1)


def finish_mix(density, base_density, dens_hist, resid_hist, summed):
    gram = summed[:, :-1]
    projections = summed[:, -1]
    system = gram + regular * jnp.diag(jnp.diag(gram))
    chol_factor = jnp.linalg.cholesky(system)
    mix_coefs = jax.scipy.linalg.cho_solve((chol_factor, True), projections)
    update = jnp.einsum(
        "h,hzxy->zxy", mix_coefs, dens_hist + beta_mix * resid_hist, precision=highest
    )
    return base_density + beta_mix * (density - base_density) - update


def shards(psi_hat, occupations, weights, density_in, dens_hist, resid_hist):
    cosine_table, sine_table = dft_tables()
    weight_total = lax.psum(jnp.sum(weights.astype(jnp.float32)), "ka")
    after_kz = rotate("bpqk,kz->bzpq", psi_hat[0, :, 0], psi_hat[0, :, 1], cosine_table, sine_table)
    after_ky = rotate("bzpq,qy->bzpy", after_kz[0], after_kz[1], cosine_table, sine_table)
    stacked = jnp.stack(after_ky, axis=1)
    received = lax.all_to_all(stacked, "band", split_axis=2, concat_axis=3, tiled=True)
    real_part, imag_part = rotate(
        "bzpy,px->bzxy", received[:, 0], received[:, 1], cosine_table, sine_table
    )
    power = (real_part * real_part + imag_part * imag_part) * jnp.float32(1.0 / NG**3)
    occ_float = occupations[0].astype(jnp.float32)
    pool_term = jnp.einsum("b,bzxy->zxy", occ_float, power, precision=highest)
    pool_term = pool_term * (weights[0].astype(jnp.float32) / weight_total)
    share = lax.psum_scatter(pool_term, "ka", scatter_dimension=1, tiled=True)
    share_width = share.shape[1]
    share_start = lax.axis_index("ka") * share_width
    base_density = lax.dynamic_slice_in_dim(density_in, share_start, share_width, 1)
    dens_part = lax.dynamic_slice_in_dim(dens_hist, share_start, share_width, 2)
    resid_part = lax.dynamic_slice_in_dim(resid_hist, share_start, share_width, 2)
    partial_terms = local_sums(share - base_density, resid_part)
    summed = lax.psum(partial_terms, ("ka", "band"))
    mixed_share = finish_mix(share, base_density, dens_part, resid_part, summed)
    density, mixed_density = (
        lax.all_gather(share, "ka", axis=1, tiled=True),
        lax.all_gather(mixed_share, "ka", axis=1, tiled=True),
    )
    return (density, mixed_density)


def solution(mesh):
    return jax.shard_map(
        shards,
        mesh=mesh,
        in_specs=(
            P("ka", None, None, "band", None, None),
            P("ka", None),
            P("ka"),
            P("band", None, None),
            P(None, "band", None, None),
            P(None, "band", None, None),
        ),
        out_specs=(P("band", None, None), P("band", None, None)),
        check_vma=False,
    )
```

profile of v0, /device:TPU:0, one launch (start us, length us, event | category | flops | bytes accessed | tf_op | source)
XLA Modules:
  0.0 529.3 jit_solution(17351105606221677500)
XLA Ops:
  7.2 0.0 copy-start.1
  7.2 8.3 %fusion.2 = f32[128,12,8,128]{3,0,2,1:T(8,128)S(1)} fusion(f32[1,12,2,8,128,128]{5,4,3,2,1,0:T(8,128)} %param.6), kind=kOutput, calls=%fused_computation.7 | convolution fusion | flops 2416148480 | bytes 12582912 | tf_op jit(solution)/shard_map/bpqk,kz->bzpq/dot_general | solution.py:23
  15.5 0.0 copy-done.1
  15.5 6.2 %fusion.6 = f32[128,12,8,128]{3,0,2,1:T(8,128)S(1)} fusion(f32[1,12,2,8,128,128]{5,4,3,2,1,0:T(8,128)S(1)} %copy-done.1), kind=kOutput, calls=%fused_computation.11 | convolution fusion | flops 2416148480 | bytes 12582912 | tf_op jit(solution)/shard_map/bpqk,kz->bzpq/dot_general | solution.py:23
  21.7 8.7 %fusion.4 = f32[128,12,8,128]{3,0,2,1:T(8,128)S(1)} fusion(f32[1,12,2,8,128,128]{5,4,3,2,1,0:T(8,128)} %param.6), kind=kOutput, calls=%fused_computation.9 | convolution fusion | flops 2416148480 | bytes 12582912 | tf_op jit(solution)/shard_map/bpqk,kz->bzpq/dot_general | solution.py:22
  30.3 8.1 %fusion.8 = f32[128,12,8,128]{3,0,2,1:T(8,128)S(1)} fusion(f32[1,12,2,8,128,128]{5,4,3,2,1,0:T(8,128)} %param.6), kind=kOutput, calls=%fused_computation.13 | convolution fusion | flops 2416148480 | bytes 12582912 | tf_op jit(solution)/shard_map/bpqk,kz->bzpq/dot_general | solution.py:22
  38.5 7.4 %fusion.10 = f32[12,128,8,128]{3,1,2,0:T(8,128)} fusion(f32[128,12,8,128]{3,0,2,1:T(8,128)S(1)} %fusion.6, f32[128,12,8,128]{3,0,2,1:T(8,128)S(1)} %fusion.2), kind=kOutput, calls=%fused_computation.15 | convolution fusion | flops 2417721344 | bytes 18874368 | tf_op jit(solution)/shard_map/bzpq,qy->bzpy/dot_general | solution.py:23
  45.8 7.7 %fusion.12 = f32[12,128,8,128]{3,1,2,0:T(8,128)} fusion(f32[128,12,8,128]{3,0,2,1:T(8,128)S(1)} %fusion.6, f32[128,12,8,128]{3,0,2,1:T(8,128)S(1)} %fusion.2), kind=kOutput, calls=%fused_computation.17 | convolution fusion | flops 2417721344 | bytes 18874368 | tf_op jit(solution)/shard_map/bzpq,qy->bzpy/dot_general | solution.py:22
  53.5 0.0 copy-start.2
  53.5 8.2 %add_bitcast_fusion = f32[12,1,128,8,128]{4,2,3,0,1:T(8,128)S(1)} fusion(f32[12,128,8,128]{3,1,2,0:T(8,128)} %fusion.10, f32[128,12,8,128]{3,0,2,1:T(8,128)S(1)} %fusion.8, f32[128,12,8,128]{3,0,2,1:T(8,128)S(1)} %fusion.4), kind=kOutput, calls=%fused_computation.24 | convolution fusion | flops 2419294208 | bytes 25165824 | tf_op jit(solution)/shard_map/bzpq,qy->bzpy/dot_general | solution.py:23
  61.7 0.0 copy-done.2
  61.7 7.7 %subtract_bitcast_fusion = f32[12,1,128,8,128]{4,2,3,0,1:T(8,128)} fusion(f32[12,128,8,128]{3,1,2,0:T(8,128)S(1)} %copy-done.2, f32[128,12,8,128]{3,0,2,1:T(8,128)S(1)} %fusion.8, f32[128,12,8,128]{3,0,2,1:T(8,128)S(1)} %fusion.4), kind=kOutput, calls=%fused_computation.25 | convolution fusion | flops 2419294208 | bytes 25165824 | tf_op jit(solution)/shard_map/bzpq,qy->bzpy/dot_general | solution.py:22
  69.4 9.0 %pad_maximum_fusion = f32[12,2,128,8,128]{4,2,3,0,1:T(8,128)} fusion(f32[12,1,128,8,128]{4,2,3,0,1:T(8,128)S(1)} %add_bitcast_fusion, f32[12,1,128,8,128]{4,2,3,0,1:T(8,128)} %subtract_bitcast_fusion), kind=kLoop, calls=%fused_computation.1 | loop fusion | flops 3145728 | bytes 25165824 | tf_op jit(solution)/shard_map/stack | solution.py:53
  78.4 16.3 %copy.60 = f32[12,2,128,8,128]{4,3,0,1,2:T(8,128)} copy(f32[12,2,128,8,128]{4,2,3,0,1:T(8,128)} %pad_maximum_fusion) | data formatting | bytes 25165824 | tf_op jit(solution)/shard_map/stack | solution.py:53
  94.8 7.5 %all-to-all-start = ((f32[12,2,128,8,128]{4,3,0,1,2:T(8,128)}), f32[12,2,128,8,128]{4,3,0,1,2:T(8,128)}, u32[]{:S(2)}, u32[]{:S(2)}) async-start(f32[12,2,128,8,128]{4,3,0,1,2:T(8,128)} %copy.60), calls=%async_computation | async-start | bytes 25165824 | tf_op jit(solution)/shard_map/all_to_all | solution.py:54
  102.2 0.0 reduce-scatter.2.cloned.1.call-start
  102.9 6.1 %psum.14 = f32[]{:T(128)} all-reduce(f32[]{:T(128)} %bitcast.28), channel_id=1, replica_groups=mesh['ka'=2,'band'=16] {'ka'}, use_global_device_ids=true, to_apply=%region_0.1 | all-reduce | flops 1 | bytes 8 | tf_op jit(solution)/shard_map/psum | solution.py:50
  109.7 216.1 %all-to-all-done = f32[12,2,128,8,128]{4,3,0,1,2:T(8,128)} async-done(((f32[12,2,128,8,128]{4,3,0,1,2:T(8,128)}), f32[12,2,128,8,128]{4,3,0,1,2:T(8,128)}, u32[]{:S(2)}, u32[]{:S(2)}) %all-to-all-start) | async-done | bytes 12582944 | tf_op jit(solution)/shard_map/all_to_all | solution.py:54
  325.8 10.8 %copy.121 = f32[12,2,8,16,8,128]{5,4,3,2,1,0:T(8,128)} copy(f32[12,2,8,16,8,128]{5,4,0,1,2,3:T(8,128)} %bitcast.18) | data formatting | bytes 25165824 | tf_op jit(solution)/shard_map/all_to_all | solution.py:54
  336.7 0.0 copy-start
  336.7 10.2 %fusion.18 = f32[128,12,8,128]{3,0,2,1:T(8,128)} fusion(f32[12,2,8,128,128]{4,3,2,1,0:T(8,128)} %bitcast.136), kind=kOutput, calls=%fused_computation.26 | convolution fusion | flops 2416148480 | bytes 12582912 | tf_op jit(solution)/shard_map/bzpy,px->bzxy/dot_general | solution.py:23
  346.9 0.0 copy-done
  346.9 7.8 %fusion.19 = f32[128,12,8,128]{3,0,2,1:T(8,128)} fusion(f32[12,2,8,128,128]{4,3,2,1,0:T(8,128)S(1)} %bitcast.137), kind=kOutput, calls=%fused_computation.27 | convolution fusion | flops 2416148480 | bytes 12582912 | tf_op jit(solution)/shard_map/bzpy,px->bzxy/dot_general | solution.py:22
  354.7 7.8 %fusion.20 = f32[128,12,8,128]{3,0,2,1:T(8,128)} fusion(f32[12,2,8,128,128]{4,3,2,1,0:T(8,128)S(1)} %bitcast.138), kind=kOutput, calls=%fused_computation.28 | convolution fusion | flops 2416148480 | bytes 12582912 | tf_op jit(solution)/shard_map/bzpy,px->bzxy/dot_general | solution.py:23
  362.4 0.0 copy-start.5
  362.4 11.7 %multiply_bitcast_fusion = f32[12,8,128,128]{3,2,1,0:T(8,128)S(1)} fusion(f32[128,12,8,128]{3,0,2,1:T(8,128)} %fusion.18, f32[128,12,8,128]{3,0,2,1:T(8,128)} %fusion.20, f32[128,12,8,128]{3,0,2,1:T(8,128)} %fusion.19, f32[12,2,8,128,128]{4,3,2,1,0:T(8,128)S(1)} %bitcast.139), kind=kOutput, calls=%fused_computation.23 | convolution fusion | flops 2425585664 | bytes 31457280 | tf_op jit(solution)/shard_map/bzpy,px->bzxy/dot_general | solution.py:22
  374.1 0.0 copy-done.5
  374.1 10.8 %fusion = f32[1,8,128,128]{3,0,2,1:T(1,128)S(1)} fusion(f32[12,8,128,128]{3,2,1,0:T(8,128)S(1)} %multiply_bitcast_fusion, s32[1,12]{1,0:T(1,128)S(1)} %copy-done.5), kind=kOutput, calls=%fused_computation.3 | convolution fusion | flops 18874380 | bytes 6815792 | tf_op jit(solution)/shard_map/b,bzxy->zxy/dot_general | solution.py:60
  384.9 0.0 copy-start.4
  384.9 0.8 broadcast_multiply_fusion
  385.8 0.0 reduce-scatter.2.cloned.1.call-update
  385.8 1.7 constant_dynamic-slice_fusion.1
  387.5 3.2 constant_dynamic-slice_fusion
  390.8 4.9 fusion.40
  395.6 53.6 %reduce-scatter.2.cloned.1.call-done = f32[8,64,128]{2,1,0:T(8,128)} async-done(((f32[8,128,128]{2,1,0:T(8,128)}), f32[8,64,128]{2,1,0:T(8,128)}) %reduce-scatter.2.cloned.1.call-update) | async-done | bytes 262160 | tf_op jit(solution)/shard_map/reduce_scatter | solution.py:62
  449.3 0.0 copy-done.4
  449.3 0.0 copy-start.3
  449.3 1.1 fusion.47
  450.3 5.2 fusion.43
  455.6 39.6 %psum.15 = f32[8,9]{0,1:T(8,128)S(1)} all-reduce(f32[8,9]{0,1:T(8,128)S(1)} %pad_maximum_fusion.1), channel_id=1, replica_groups=mesh['ka'=2,'band'=16] {'ka','band'}, use_global_device_ids=true, to_apply=%region_2.3 | all-reduce | flops 72 | bytes 576 | tf_op jit(solution)/shard_map/psum | solution.py:69
  495.2 0.6 gather_fusion
  495.8 0.1 copy.67
  495.9 0.7 cholesky.16
  496.6 0.1 copy.68
  496.7 0.2 select_reduce_fusion
  496.8 0.6 compare_reduce_fusion
  497.5 0.6 select_select_fusion
  498.1 0.1 copy.70
  498.2 0.6 custom-call.10
  498.8 0.1 convolution_bitcast_fusion.1
  499.0 0.1 convolution_bitcast_fusion
  499.1 5.7 %fusion.34 = f32[1,8,64,128]{3,0,2,1:T(1,128)S(1)} fusion(f32[8,1,1,1]{0,1,3,2:T(1,128)S(1)} %convolution_bitcast_fusion, f32[8,8,64,128]{3,2,1,0:T(8,128)} %constant_dynamic-slice_fusion, f32[8,8,64,128]{3,2,1,0:T(8,128)S(1)} %constant_dynamic-slice_fusion.1), kind=kOutput, calls=%fused_computation.39 | convolution fusion | flops 7340032 | bytes 4456480 | tf_op jit(solution)/shard_map/h,hzxy->zxy/dot_general | solution.py:42
  504.8 0.0 copy-done.3
  504.8 0.1 add_subtract_fusion
  504.9 8.4 %all_gather.7 = f32[8,128,128]{2,1,0:T(8,128)S(1)} all-gather(f32[8,64,128]{2,1,0:T(8,128)S(1)} %add_subtract_fusion), channel_id=1, replica_groups=mesh['ka'=2,'band'=16] {'ka'}, dimensions={1}, use_global_device_ids=true | all-gather | bytes 786432 | tf_op jit(solution)/shard_map/all_gather | solution.py:73
  513.3 7.3 %all_gather.6 = f32[8,128,128]{2,1,0:T(8,128)S(1)} all-gather(f32[8,64,128]{2,1,0:T(8,128)S(1)} %copy-done.3), channel_id=1, replica_groups=mesh['ka'=2,'band'=16] {'ka'}, dimensions={1}, use_global_device_ids=true | all-gather | bytes 786432 | tf_op jit(solution)/shard_map/all_gather | solution.py:72
  520.6 0.8 copy.125
  521.4 0.8 copy.126
  (5 shorter events, 0.0 us)
Async XLA Ops:
  7.2 8.3 %copy-start.1 = (f32[1,12,2,8,128,128]{5,4,3,2,1,0:T(8,128)S(1)}, f32[1,12,2,8,128,128]{5,4,3,2,1,0:T(8,128)}, u32[]{:S(2)}) copy-start(f32[1,12,2,8,128,128]{5,4,3,2,1,0:T(8,128)} %param.6) | copy-start | bytes 37748740
  53.5 8.2 %copy-start.2 = (f32[12,128,8,128]{3,1,2,0:T(8,128)S(1)}, f32[12,128,8,128]{3,1,2,0:T(8,128)}, u32[]{:S(2)}) copy-start(f32[12,128,8,128]{3,1,2,0:T(8,128)} %fusion.12) | copy-start | bytes 18874372
  94.8 231.1 %all-to-all-start = ((f32[12,2,128,8,128]{4,3,0,1,2:T(8,128)}), f32[12,2,128,8,128]{4,3,0,1,2:T(8,128)}, u32[]{:S(2)}, u32[]{:S(2)}) async-start(f32[12,2,128,8,128]{4,3,0,1,2:T(8,128)} %copy.60), calls=%async_computation | async-start | bytes 25165824 | tf_op jit(solution)/shard_map/all_to_all | solution.py:54
  102.2 347.0 %reduce-scatter.2.cloned.1.call-start = ((), (), s32[]{:S(2)}) async-start(), calls=%async_computation.2 | async-start | bytes 786432 | tf_op jit(solution)/shard_map/reduce_scatter | solution.py:62
  336.7 10.2 %copy-start = (f32[12,2,8,16,8,128]{5,4,3,2,1,0:T(8,128)S(1)}, f32[12,2,8,16,8,128]{5,4,3,2,1,0:T(8,128)}, u32[]{:S(2)}) copy-start(f32[12,2,8,16,8,128]{5,4,3,2,1,0:T(8,128)} %copy.121) | copy-start | bytes 37748740
  362.4 11.7 %copy-start.5 = (s32[1,12]{1,0:T(1,128)S(1)}, s32[1,12]{1,0:T(1,128)}, u32[]{:S(2)}) copy-start(s32[1,12]{1,0:T(1,128)} %param.7) | copy-start | bytes 148
  384.9 64.4 %copy-start.4 = (f32[8,128,128]{2,1,0:T(8,128)S(1)}, f32[8,128,128]{2,1,0:T(8,128)}, u32[]{:S(2)}) copy-start(f32[8,128,128]{2,1,0:T(8,128)} %param.9) | copy-start | bytes 1572868
  449.3 55.5 %copy-start.3 = (f32[8,64,128]{2,1,0:T(8,128)S(1)}, f32[8,64,128]{2,1,0:T(8,128)}, u32[]{:S(2)}) copy-start(f32[8,64,128]{2,1,0:T(8,128)} %reduce-scatter.2.cloned.1.call-done) | copy-start | bytes 786436
Sparse Core Ops, SparseCore 0:
  385.9 63.3 reduce-scatter.1
where the time goes:
time: 536 us; the launch traced here: 529 us
  waiting for transfers between devices  270 us (50%)
  matrix products  126 us (24%)
  blocking collectives  61.5 us (11%)
  local copies, waits for them, and re-layouts  34.6 us (6%)
  between operations  15.8 us (3%)
  other arithmetic  13.8 us (3%)
  starting transfers between devices  7.5 us (1%)
    all_to_all x1, waiting for transfers between devices, shards(): lax.all_to_all(stacked, 'band', split_axis=2, concat_axis=3, tiled=True)  216 us
    reduce_scatter x1, waiting for transfers between devices, shards(): share = lax.psum_scatter(pool_term, 'ka', scatter_dimension=1, tiled=True)  53.6 us
    psum x1, blocking collectives, shards(): summed = lax.psum(partial_terms, ('ka', 'band'))  39.6 us
    dot_general x3, matrix products, rotate(): einsum(pattern, imag_part, sine_table)  28 us
    dot_general x3, matrix products, rotate(): einsum(pattern, real_part, sine_table)  24.6 us
    dot_general x3, matrix products, rotate(): einsum(pattern, real_part, cosine_table)  23.6 us
    dot_general x3, matrix products, rotate(): einsum(pattern, imag_part, cosine_table)  23.4 us
    another operation x1, local copies, waits for them, and re-layouts, shards(): stacked = jnp.stack(after_ky, axis=1)  16.3 us
  transfers between devices with their start and end apart: 2, of which 2 were waited for; matrix products, arithmetic and copies ran while one was open for 2% of the time, Pallas kernels for 0%

commit v1 on v0

--- a/solution.py
+++ b/solution.py
@@ -66,7 +66,7 @@
     dens_part = lax.dynamic_slice_in_dim(dens_hist, share_start, share_width, 2)
     resid_part = lax.dynamic_slice_in_dim(resid_hist, share_start, share_width, 2)
     partial_terms = local_sums(share - base_density, resid_part)
-    summed = lax.psum(partial_terms, ("ka", "band"))
+    summed = lax.psum(lax.psum(partial_terms, "band"), "ka")
     mixed_share = finish_mix(share, base_density, dens_part, resid_part, summed)
     density, mixed_density = (
         lax.all_gather(share, "ka", axis=1, tiled=True),

time: 536 us -> 537 us (level)
    psum x1 -> x2, blocking collectives: 39.6 us -> 38.8 us  [shards(): summed = lax.psum(lax.psum(partial_terms, 'band'), 'ka')]
where the time goes in v1:
time: 537 us; the launch traced here: 530 us
  waiting for transfers between devices  270 us (50%)
  matrix products  126 us (23%)
  blocking collectives  61.7 us (11%)
  local copies, waits for them, and re-layouts  34.6 us (6%)
  between operations  15.8 us (3%)
  other arithmetic  13.8 us (3%)
  starting transfers between devices  7.5 us (1%)
    all_to_all x1, waiting for transfers between devices, shards(): lax.all_to_all(stacked, 'band', split_axis=2, concat_axis=3, tiled=True)  216 us
    reduce_scatter x1, waiting for transfers between devices, shards(): share = lax.psum_scatter(pool_term, 'ka', scatter_dimension=1, tiled=True)  53.6 us
    psum x2, blocking collectives, shards(): summed = lax.psum(lax.psum(partial_terms, 'band'), 'ka')  38.8 us
    dot_general x3, matrix products, rotate(): einsum(pattern, imag_part, sine_table)  28 us
    dot_general x3, matrix products, rotate(): einsum(pattern, real_part, sine_table)  24.6 us
    dot_general x3, matrix products, rotate(): einsum(pattern, real_part, cosine_table)  23.6 us
    dot_general x3, matrix products, rotate(): einsum(pattern, imag_part, cosine_table)  23.4 us
    another operation x1, local copies, waits for them, and re-layouts, shards(): stacked = jnp.stack(after_ky, axis=1)  16.3 us
  transfers between devices with their start and end apart: 2, of which 2 were waited for; matrix products, arithmetic and copies ran while one was open for 2% of the time, Pallas kernels for 0%

profile of v1, /device:TPU:0, one launch (start us, length us, event | category | flops | bytes accessed | tf_op | source)
XLA Modules:
  0.0 529.5 jit_solution(9208165874949613434)
XLA Ops:
  7.2 0.0 copy-start.1
  7.2 8.3 %fusion.2 = f32[128,12,8,128]{3,0,2,1:T(8,128)S(1)} fusion(f32[1,12,2,8,128,128]{5,4,3,2,1,0:T(8,128)} %param.6), kind=kOutput, calls=%fused_computation.7 | convolution fusion | flops 2416148480 | bytes 12582912 | tf_op jit(solution)/shard_map/bpqk,kz->bzpq/dot_general | solution.py:23
  15.5 0.0 copy-done.1
  15.5 6.2 %fusion.6 = f32[128,12,8,128]{3,0,2,1:T(8,128)S(1)} fusion(f32[1,12,2,8,128,128]{5,4,3,2,1,0:T(8,128)S(1)} %copy-done.1), kind=kOutput, calls=%fused_computation.11 | convolution fusion | flops 2416148480 | bytes 12582912 | tf_op jit(solution)/shard_map/bpqk,kz->bzpq/dot_general | solution.py:23
  21.7 8.7 %fusion.4 = f32[128,12,8,128]{3,0,2,1:T(8,128)S(1)} fusion(f32[1,12,2,8,128,128]{5,4,3,2,1,0:T(8,128)} %param.6), kind=kOutput, calls=%fused_computation.9 | convolution fusion | flops 2416148480 | bytes 12582912 | tf_op jit(solution)/shard_map/bpqk,kz->bzpq/dot_general | solution.py:22
  30.3 8.1 %fusion.8 = f32[128,12,8,128]{3,0,2,1:T(8,128)S(1)} fusion(f32[1,12,2,8,128,128]{5,4,3,2,1,0:T(8,128)} %param.6), kind=kOutput, calls=%fused_computation.13 | convolution fusion | flops 2416148480 | bytes 12582912 | tf_op jit(solution)/shard_map/bpqk,kz->bzpq/dot_general | solution.py:22
  38.5 7.4 %fusion.10 = f32[12,128,8,128]{3,1,2,0:T(8,128)} fusion(f32[128,12,8,128]{3,0,2,1:T(8,128)S(1)} %fusion.6, f32[128,12,8,128]{3,0,2,1:T(8,128)S(1)} %fusion.2), kind=kOutput, calls=%fused_computation.15 | convolution fusion | flops 2417721344 | bytes 18874368 | tf_op jit(solution)/shard_map/bzpq,qy->bzpy/dot_general | solution.py:23
  45.8 7.7 %fusion.12 = f32[12,128,8,128]{3,1,2,0:T(8,128)} fusion(f32[128,12,8,128]{3,0,2,1:T(8,128)S(1)} %fusion.6, f32[128,12,8,128]{3,0,2,1:T(8,128)S(1)} %fusion.2), kind=kOutput, calls=%fused_computation.17 | convolution fusion | flops 2417721344 | bytes 18874368 | tf_op jit(solution)/shard_map/bzpq,qy->bzpy/dot_general | solution.py:22
  53.5 0.0 copy-start.2
  53.5 8.2 %add_bitcast_fusion = f32[12,1,128,8,128]{4,2,3,0,1:T(8,128)S(1)} fusion(f32[12,128,8,128]{3,1,2,0:T(8,128)} %fusion.10, f32[128,12,8,128]{3,0,2,1:T(8,128)S(1)} %fusion.8, f32[128,12,8,128]{3,0,2,1:T(8,128)S(1)} %fusion.4), kind=kOutput, calls=%fused_computation.24 | convolution fusion | flops 2419294208 | bytes 25165824 | tf_op jit(solution)/shard_map/bzpq,qy->bzpy/dot_general | solution.py:23
  61.7 0.0 copy-done.2
  61.7 7.7 %subtract_bitcast_fusion = f32[12,1,128,8,128]{4,2,3,0,1:T(8,128)} fusion(f32[12,128,8,128]{3,1,2,0:T(8,128)S(1)} %copy-done.2, f32[128,12,8,128]{3,0,2,1:T(8,128)S(1)} %fusion.8, f32[128,12,8,128]{3,0,2,1:T(8,128)S(1)} %fusion.4), kind=kOutput, calls=%fused_computation.25 | convolution fusion | flops 2419294208 | bytes 25165824 | tf_op jit(solution)/shard_map/bzpq,qy->bzpy/dot_general | solution.py:22
  69.4 9.0 %pad_maximum_fusion = f32[12,2,128,8,128]{4,2,3,0,1:T(8,128)} fusion(f32[12,1,128,8,128]{4,2,3,0,1:T(8,128)S(1)} %add_bitcast_fusion, f32[12,1,128,8,128]{4,2,3,0,1:T(8,128)} %subtract_bitcast_fusion), kind=kLoop, calls=%fused_computation.1 | loop fusion | flops 3145728 | bytes 25165824 | tf_op jit(solution)/shard_map/stack | solution.py:53
  78.4 16.3 %copy.60 = f32[12,2,128,8,128]{4,3,0,1,2:T(8,128)} copy(f32[12,2,128,8,128]{4,2,3,0,1:T(8,128)} %pad_maximum_fusion) | data formatting | bytes 25165824 | tf_op jit(solution)/shard_map/stack | solution.py:53
  94.8 7.5 %all-to-all-start = ((f32[12,2,128,8,128]{4,3,0,1,2:T(8,128)}), f32[12,2,128,8,128]{4,3,0,1,2:T(8,128)}, u32[]{:S(2)}, u32[]{:S(2)}) async-start(f32[12,2,128,8,128]{4,3,0,1,2:T(8,128)} %copy.60), calls=%async_computation | async-start | bytes 25165824 | tf_op jit(solution)/shard_map/all_to_all | solution.py:54
  102.2 0.0 reduce-scatter.2.cloned.1.call-start
  102.9 6.1 %psum.21 = f32[]{:T(128)} all-reduce(f32[]{:T(128)} %bitcast.28), channel_id=1, replica_groups=mesh['ka'=2,'band'=16] {'ka'}, use_global_device_ids=true, to_apply=%region_0.1 | all-reduce | flops 1 | bytes 8 | tf_op jit(solution)/shard_map/psum | solution.py:50
  109.7 216.1 %all-to-all-done = f32[12,2,128,8,128]{4,3,0,1,2:T(8,128)} async-done(((f32[12,2,128,8,128]{4,3,0,1,2:T(8,128)}), f32[12,2,128,8,128]{4,3,0,1,2:T(8,128)}, u32[]{:S(2)}, u32[]{:S(2)}) %all-to-all-start) | async-done | bytes 12582944 | tf_op jit(solution)/shard_map/all_to_all | solution.py:54
  325.8 10.8 %copy.121 = f32[12,2,8,16,8,128]{5,4,3,2,1,0:T(8,128)} copy(f32[12,2,8,16,8,128]{5,4,0,1,2,3:T(8,128)} %bitcast.18) | data formatting | bytes 25165824 | tf_op jit(solution)/shard_map/all_to_all | solution.py:54
  336.7 0.0 copy-start
  336.7 10.2 %fusion.18 = f32[128,12,8,128]{3,0,2,1:T(8,128)} fusion(f32[12,2,8,128,128]{4,3,2,1,0:T(8,128)} %bitcast.136), kind=kOutput, calls=%fused_computation.26 | convolution fusion | flops 2416148480 | bytes 12582912 | tf_op jit(solution)/shard_map/bzpy,px->bzxy/dot_general | solution.py:23
  346.9 0.0 copy-done
  346.9 7.8 %fusion.19 = f32[128,12,8,128]{3,0,2,1:T(8,128)} fusion(f32[12,2,8,128,128]{4,3,2,1,0:T(8,128)S(1)} %bitcast.137), kind=kOutput, calls=%fused_computation.27 | convolution fusion | flops 2416148480 | bytes 12582912 | tf_op jit(solution)/shard_map/bzpy,px->bzxy/dot_general | solution.py:22
  354.7 7.8 %fusion.20 = f32[128,12,8,128]{3,0,2,1:T(8,128)} fusion(f32[12,2,8,128,128]{4,3,2,1,0:T(8,128)S(1)} %bitcast.138), kind=kOutput, calls=%fused_computation.28 | convolution fusion | flops 2416148480 | bytes 12582912 | tf_op jit(solution)/shard_map/bzpy,px->bzxy/dot_general | solution.py:23
  362.4 0.0 copy-start.5
  362.4 11.7 %multiply_bitcast_fusion = f32[12,8,128,128]{3,2,1,0:T(8,128)S(1)} fusion(f32[128,12,8,128]{3,0,2,1:T(8,128)} %fusion.18, f32[128,12,8,128]{3,0,2,1:T(8,128)} %fusion.20, f32[128,12,8,128]{3,0,2,1:T(8,128)} %fusion.19, f32[12,2,8,128,128]{4,3,2,1,0:T(8,128)S(1)} %bitcast.139), kind=kOutput, calls=%fused_computation.23 | convolution fusion | flops 2425585664 | bytes 31457280 | tf_op jit(solution)/shard_map/bzpy,px->bzxy/dot_general | solution.py:22
  374.1 0.0 copy-done.5
  374.1 10.8 %fusion = f32[1,8,128,128]{3,0,2,1:T(1,128)S(1)} fusion(f32[12,8,128,128]{3,2,1,0:T(8,128)S(1)} %multiply_bitcast_fusion, s32[1,12]{1,0:T(1,128)S(1)} %copy-done.5), kind=kOutput, calls=%fused_computation.3 | convolution fusion | flops 18874380 | bytes 6815792 | tf_op jit(solution)/shard_map/b,bzxy->zxy/dot_general | solution.py:60
  384.9 0.0 copy-start.4
  384.9 0.8 broadcast_multiply_fusion
  385.8 0.0 reduce-scatter.2.cloned.1.call-update
  385.8 1.7 constant_dynamic-slice_fusion.1
  387.5 3.2 constant_dynamic-slice_fusion
  390.8 4.9 fusion.40
  395.6 53.6 %reduce-scatter.2.cloned.1.call-done = f32[8,64,128]{2,1,0:T(8,128)} async-done(((f32[8,128,128]{2,1,0:T(8,128)}), f32[8,64,128]{2,1,0:T(8,128)}) %reduce-scatter.2.cloned.1.call-update) | async-done | bytes 262160 | tf_op jit(solution)/shard_map/reduce_scatter | solution.py:62
  449.3 0.0 copy-done.4
  449.3 0.0 copy-start.3
  449.3 1.1 fusion.47
  450.3 5.2 fusion.43
  455.6 33.5 %psum.22 = f32[8,9]{0,1:T(8,128)S(1)} all-reduce(f32[8,9]{0,1:T(8,128)S(1)} %pad_maximum_fusion.1), channel_id=1, replica_groups=mesh['ka'=2,'band'=16] {'band'}, use_global_device_ids=true, to_apply=%region_2.3 | all-reduce | flops 72 | bytes 576 | tf_op jit(solution)/shard_map/psum | solution.py:69
  489.1 5.2 psum.23
  494.3 0.6 gather_fusion
  495.0 0.1 copy.67
  495.1 0.7 cholesky.16
  495.8 0.1 copy.68
  495.8 0.2 select_reduce_fusion
  496.0 0.6 compare_reduce_fusion
  496.6 0.6 select_select_fusion
  497.3 0.1 copy.70
  497.4 0.6 custom-call.10
  498.0 0.1 convolution_bitcast_fusion.1
  498.1 0.1 convolution_bitcast_fusion
  498.3 5.7 %fusion.34 = f32[1,8,64,128]{3,0,2,1:T(1,128)S(1)} fusion(f32[8,1,1,1]{0,1,3,2:T(1,128)S(1)} %convolution_bitcast_fusion, f32[8,8,64,128]{3,2,1,0:T(8,128)} %constant_dynamic-slice_fusion, f32[8,8,64,128]{3,2,1,0:T(8,128)S(1)} %constant_dynamic-slice_fusion.1), kind=kOutput, calls=%fused_computation.39 | convolution fusion | flops 7340032 | bytes 4456480 | tf_op jit(solution)/shard_map/h,hzxy->zxy/dot_general | solution.py:42
  503.9 0.0 copy-done.3
  503.9 0.1 add_subtract_fusion
  504.0 9.8 %all_gather.7 = f32[8,128,128]{2,1,0:T(8,128)S(1)} all-gather(f32[8,64,128]{2,1,0:T(8,128)S(1)} %add_subtract_fusion), channel_id=1, replica_groups=mesh['ka'=2,'band'=16] {'ka'}, dimensions={1}, use_global_device_ids=true | all-gather | bytes 786432 | tf_op jit(solution)/shard_map/all_gather | solution.py:73
  513.8 7.0 %all_gather.6 = f32[8,128,128]{2,1,0:T(8,128)S(1)} all-gather(f32[8,64,128]{2,1,0:T(8,128)S(1)} %copy-done.3), channel_id=1, replica_groups=mesh['ka'=2,'band'=16] {'ka'}, dimensions={1}, use_global_device_ids=true | all-gather | bytes 786432 | tf_op jit(solution)/shard_map/all_gather | solution.py:72
  520.8 0.8 copy.125
  521.6 0.8 copy.126
  (5 shorter events, 0.0 us)
Async XLA Ops:
  7.2 8.3 %copy-start.1 = (f32[1,12,2,8,128,128]{5,4,3,2,1,0:T(8,128)S(1)}, f32[1,12,2,8,128,128]{5,4,3,2,1,0:T(8,128)}, u32[]{:S(2)}) copy-start(f32[1,12,2,8,128,128]{5,4,3,2,1,0:T(8,128)} %param.6) | copy-start | bytes 37748740
  53.5 8.2 %copy-start.2 = (f32[12,128,8,128]{3,1,2,0:T(8,128)S(1)}, f32[12,128,8,128]{3,1,2,0:T(8,128)}, u32[]{:S(2)}) copy-start(f32[12,128,8,128]{3,1,2,0:T(8,128)} %fusion.12) | copy-start | bytes 18874372
  94.8 231.1 %all-to-all-start = ((f32[12,2,128,8,128]{4,3,0,1,2:T(8,128)}), f32[12,2,128,8,128]{4,3,0,1,2:T(8,128)}, u32[]{:S(2)}, u32[]{:S(2)}) async-start(f32[12,2,128,8,128]{4,3,0,1,2:T(8,128)} %copy.60), calls=%async_computation | async-start | bytes 25165824 | tf_op jit(solution)/shard_map/all_to_all | solution.py:54
  102.2 347.0 %reduce-scatter.2.cloned.1.call-start = ((), (), s32[]{:S(2)}) async-start(), calls=%async_computation.2 | async-start | bytes 786432 | tf_op jit(solution)/shard_map/reduce_scatter | solution.py:62
  336.7 10.2 %copy-start = (f32[12,2,8,16,8,128]{5,4,3,2,1,0:T(8,128)S(1)}, f32[12,2,8,16,8,128]{5,4,3,2,1,0:T(8,128)}, u32[]{:S(2)}) copy-start(f32[12,2,8,16,8,128]{5,4,3,2,1,0:T(8,128)} %copy.121) | copy-start | bytes 37748740
  362.4 11.7 %copy-start.5 = (s32[1,12]{1,0:T(1,128)S(1)}, s32[1,12]{1,0:T(1,128)}, u32[]{:S(2)}) copy-start(s32[1,12]{1,0:T(1,128)} %param.7) | copy-start | bytes 148
  384.9 64.4 %copy-start.4 = (f32[8,128,128]{2,1,0:T(8,128)S(1)}, f32[8,128,128]{2,1,0:T(8,128)}, u32[]{:S(2)}) copy-start(f32[8,128,128]{2,1,0:T(8,128)} %param.9) | copy-start | bytes 1572868
  449.3 54.7 %copy-start.3 = (f32[8,64,128]{2,1,0:T(8,128)S(1)}, f32[8,64,128]{2,1,0:T(8,128)}, u32[]{:S(2)}) copy-start(f32[8,64,128]{2,1,0:T(8,128)} %reduce-scatter.2.cloned.1.call-done) | copy-start | bytes 786436
Sparse Core Ops, SparseCore 0:
  385.9 63.3 reduce-scatter.1
